TPU v7x, 16 devices: a whole 2x2x2 slice. The times are simulated.
16 devices in a mesh: dp: 4 (over z, y), ep: 4 (over x, core).
Axes of the slice: x: 2, y: 2, z: 2, core: 2. Of those that a mesh axis runs over, the one named last changes fastest.
Arguments:
- x: bfloat16 [131072, 1024], P(('dp', 'ep'))
- gy: bfloat16 [131072, 1024], P(('dp', 'ep'))
- idx: int32 [131072], P(('dp', 'ep'))
- w_gate: bfloat16 [1024, 32], replicated
- w_up: bfloat16 [32, 1024, 512], P('ep')
- w_down: bfloat16 [32, 512, 1024], P('ep')
Outputs:
- output 1: bfloat16 [131072, 1024], P(('dp', 'ep'))
- output 2: bfloat16 [131072, 1024], P(('dp', 'ep'))
- output 3: float32 [32, 1024, 512], P('ep')
- output 4: float32 [32, 512, 1024], P('ep')
- output 5: float32 [1024, 32], replicated
All inputs are finite; a program needn't handle non-finite values.
Results may differ from a plain program's by a relative error of at most 0.00656889.
Values are sent between devices in bfloat16 or wider.
A program may use at most 1 GiB of HBM per device.

v0:
```python
import jax
import jax.numpy as jnp
from jax import lax
from jax.sharding import PartitionSpec as P

PAD_FACTOR = 4


def solution(mesh):
    ep_size = mesh.shape['ep']
    tok_spec = P(('dp', 'ep'), None)
    idx_spec = P(('dp', 'ep'))
    rep_spec = P(None, None)
    exp_spec = P('ep', None, None)

    def local_step(x_loc, gy_loc, idx_loc, w_gate, w_up, w_down):
        tok_count, d_model = x_loc.shape
        n_experts = w_gate.shape[1]
        local_experts = w_up.shape[0]
        cap_rows = PAD_FACTOR * tok_count // n_experts
        onehot = idx_loc[:, None] == jnp.arange(n_experts, dtype=jnp.int32)[None, :]
        expert_count = jnp.sum(onehot, axis=0, dtype=jnp.int32)
        sort_order = jnp.argsort(idx_loc, stable=True)
        sorted_pos = jnp.argsort(sort_order)
        expert_start = jnp.cumsum(expert_count) - expert_count
        slot_k = jnp.arange(cap_rows, dtype=jnp.int32)
        slot_valid = slot_k[None, :] < expert_count[:, None]
        src_tok = sort_order[jnp.minimum(expert_start[:, None] + slot_k[None, :], tok_count - 1)]
        slot_tok = idx_loc * cap_rows + sorted_pos - expert_start[idx_loc]

        def dispatch(tok_rows):
            picked = jnp.where(slot_valid[:, :, None], tok_rows[src_tok], jnp.zeros((), tok_rows.dtype))
            picked = picked.reshape(ep_size, local_experts, cap_rows, d_model)
            return lax.all_to_all(picked, 'ep', 0, 0, tiled=True)

        def combine(expert_rows):
            returned = lax.all_to_all(expert_rows, 'ep', 1, 0, tiled=True)
            return returned.reshape(n_experts * cap_rows, d_model)[slot_tok]

        router_logit = jnp.dot(x_loc, w_gate, preferred_element_type=jnp.float32)
        router_prob = jax.nn.softmax(router_logit, axis=-1)
        gate_val = n_experts * jnp.sum(jnp.where(onehot, router_prob, 0.0), axis=1)
        recv_rows = dispatch(x_loc)
        pre_act = jnp.einsum('sekd,edf->eskf', recv_rows, w_up, preferred_element_type=jnp.float32)
        hid_full, gelu_back = jax.vjp(jax.nn.gelu, pre_act)
        hidden = hid_full.astype(jnp.bfloat16)
        expert_out = jnp.einsum('eskf,efd->eskd', hidden, w_down, preferred_element_type=jnp.float32).astype(jnp.bfloat16)
        y_tok = combine(expert_out)
        gy_full = gy_loc.astype(jnp.float32)
        moe_out = (gate_val[:, None] * y_tok.astype(jnp.float32)).astype(jnp.bfloat16)

        dy_tok = (gate_val[:, None] * gy_full).astype(jnp.bfloat16)
        recv_grad = dispatch(dy_tok)
        d_hidden = jnp.einsum('sekd,efd->eskf', recv_grad, w_down, preferred_element_type=jnp.float32)
        d_pre = gelu_back(d_hidden)[0].astype(jnp.bfloat16)
        grad_down = jnp.einsum('eskf,sekd->efd', hidden, recv_grad, preferred_element_type=jnp.float32)
        grad_up = jnp.einsum('sekd,eskf->edf', recv_rows, d_pre, preferred_element_type=jnp.float32)
        d_rows = jnp.einsum('eskf,edf->eskd', d_pre, w_up, preferred_element_type=jnp.float32).astype(jnp.bfloat16)
        dx_expert = combine(d_rows)
        d_gate = jnp.sum(gy_full * y_tok.astype(jnp.float32), axis=1)
        d_logit = ((d_gate * gate_val)[:, None] * (onehot.astype(jnp.float32) - router_prob)).astype(jnp.bfloat16)
        dx_router = jnp.einsum('te,de->td', d_logit, w_gate, preferred_element_type=jnp.float32)
        grad_x = (dx_expert.astype(jnp.float32) + dx_router).astype(jnp.bfloat16)
        grad_gate = jnp.einsum('td,te->de', x_loc, d_logit, preferred_element_type=jnp.float32)
        grad_up = lax.psum(grad_up, 'dp')
        grad_down = lax.psum(grad_down, 'dp')
        grad_gate = lax.psum(grad_gate, ('dp', 'ep'))
        return moe_out, grad_x, grad_up, grad_down, grad_gate

    sharded_fn = jax.shard_map(local_step, mesh=mesh, in_specs=(tok_spec, tok_spec, idx_spec, rep_spec, exp_spec, exp_spec), out_specs=(tok_spec, tok_spec, exp_spec, exp_spec, rep_spec), check_vma=False)
    return sharded_fn
```

profile of v0, /device:TPU:0, one launch (start us, length us, event | category | flops | bytes accessed | tf_op | source)
XLA Modules:
  0.0 4293.0 jit_solution(17252693671736249853)
XLA Ops:
  16.3 180.5 %gather_fusion = s32[32768]{0:T(1024)S(1)} fusion(s32[8192]{0:T(1024)S(1)} %get-tuple-element.7, s32[32768]{0:T(1024)S(1)} %broadcast_clamp_fusion), kind=kCustom, calls=%fused_computation | custom fusion | bytes 393216 | tf_op jit(solution)/shard_map/gather | solution.py:28
  197.7 167.3 %gather_fusion.1 = bf16[32768,1024]{1,0:T(8,128)(2,1)} fusion(bf16[8192,1024]{1,0:T(8,128)(2,1)} %param.6, s32[32768]{0:T(1024)S(1)} %broadcast_clamp_fusion.1), kind=kCustom, calls=%fused_computation.1 | custom fusion | bytes 134348800 | tf_op jit(solution)/shard_map/gather | solution.py:32
  365.0 44.0 %broadcast_select_fusion.1 = bf16[4,8,1024,1024]{3,2,1,0:T(8,128)(2,1)} fusion(bf16[4,8,1024,1024]{3,2,1,0:T(8,128)(2,1)} %bitcast.1, pred[4,8,1024]{2,1,0:T(8,128)(4,1)S(1)} %copy-done.23), kind=kLoop, calls=%fused_computation.18 | loop fusion | flops 33554432 | bytes 134250496 | tf_op jit(solution)/shard_map/jit(_where)/select_n | solution.py:32
  408.9 755.5 %all_to_all.40 = bf16[4,8,1024,1024]{3,2,1,0:T(8,128)(2,1)} all-to-all(bf16[4,8,1024,1024]{3,2,1,0:T(8,128)(2,1)} %broadcast_select_fusion.1), channel_id=1, replica_groups=mesh['dp'=4,'ep'=4] {'ep'}, dimensions={0} | all-to-all | bytes 134217728 | tf_op jit(solution)/shard_map/all_to_all | solution.py:34
  1164.5 58.3 %fusion.7 = f32[8,4,1024,512]{3,2,1,0:T(8,128)} fusion(bf16[4,8,1024,1024]{3,2,1,0:T(8,128)(2,1)} %all_to_all.40, bf16[8,1024,512]{2,1,0:T(8,128)(2,1)} %param.10), kind=kOutput, calls=%fused_computation.14 | convolution fusion | flops 34359738368 | bytes 142606336 | tf_op jit(solution)/shard_map/sekd,edf->eskf/dot_general | solution.py:44
  1222.8 59.9 %convolution_convert_fusion.1 = bf16[8,4,1024,1024]{3,2,1,0:T(8,128)(2,1)} fusion(bf16[8,512,1024]{2,1,0:T(8,128)(2,1)} %param.11, f32[8,4,1024,512]{3,2,1,0:T(8,128)} %fusion.7), kind=kOutput, calls=%fused_computation.24 | convolution fusion | flops 34544287744 | bytes 142606336 | tf_op jit(solution)/shard_map/eskf,efd->eskd/dot_general | solution.py:47
  1282.7 44.3 %copy.25 = bf16[8,4,1024,1024]{3,2,0,1:T(8,128)(2,1)} copy(bf16[8,4,1024,1024]{3,2,1,0:T(8,128)(2,1)} %convolution_convert_fusion.1) | data formatting | bytes 134217728 | tf_op jit(solution)/shard_map/convert_element_type | solution.py:47
  1327.0 13.6 all-to-all-start.1
  1361.6 20.0 fusion.36
  1381.6 681.0 %all-to-all-done.1 = bf16[8,4,1024,1024]{3,2,0,1:T(8,128)(2,1)} async-done(((bf16[8,4,1024,1024]{3,2,0,1:T(8,128)(2,1)}), bf16[8,4,1024,1024]{3,2,0,1:T(8,128)(2,1)}, u32[]{:S(2)}, u32[]{:S(2)}) %all-to-all-start.1) | async-done | bytes 67108896 | tf_op jit(solution)/shard_map/all_to_all | solution.py:37
  2062.6 150.2 %gather_fusion.2 = bf16[8192,1024]{1,0:T(8,128)(2,1)} fusion(bf16[32768,1024]{1,0:T(8,128)(2,1)} %bitcast.8, s32[8192]{0:T(1024)S(1)} %fusion.36), kind=kCustom, calls=%fused_computation.2 | custom fusion | bytes 33587200 | tf_op jit(solution)/shard_map/gather | solution.py:38
  2212.8 26.0 fusion.15
  2238.7 167.7 %gather_fusion.3 = bf16[32768,1024]{1,0:T(8,128)(2,1)} fusion(bf16[8192,1024]{1,0:T(8,128)(2,1)} %get-tuple-element.12, s32[32768]{0:T(1024)S(1)} %copy-done.13), kind=kCustom, calls=%fused_computation.3 | custom fusion | bytes 134348800 | tf_op jit(solution)/shard_map/gather | solution.py:32
  2406.5 44.0 %broadcast_select_fusion = bf16[4,8,1024,1024]{3,2,1,0:T(8,128)(2,1)} fusion(bf16[4,8,1024,1024]{3,2,1,0:T(8,128)(2,1)} %bitcast.41, pred[4,8,1024]{2,1,0:T(8,128)(4,1)S(1)} %copy-done.24), kind=kLoop, calls=%fused_computation.17 | loop fusion | flops 33554432 | bytes 134250496 | tf_op jit(solution)/shard_map/jit(_where)/select_n | solution.py:32
  2450.5 13.1 all-to-all-start.2
  2473.8 713.4 %all-to-all-done.2 = bf16[4,8,1024,1024]{3,2,1,0:T(8,128)(2,1)} async-done(((bf16[4,8,1024,1024]{3,2,1,0:T(8,128)(2,1)}), bf16[4,8,1024,1024]{3,2,1,0:T(8,128)(2,1)}, u32[]{:S(2)}, u32[]{:S(2)}) %all-to-all-start.2) | async-done | bytes 67108896 | tf_op jit(solution)/shard_map/all_to_all | solution.py:34
  3187.2 83.7 %fusion.6 = bf16[8,4,1024,512]{3,2,1,0:T(8,128)(2,1)} fusion(f32[8,4,1024,512]{3,2,1,0:T(8,128)} %fusion.7, bf16[8,512,1024]{2,1,0:T(8,128)(2,1)} %param.11, bf16[4,8,1024,1024]{3,2,1,0:T(8,128)(2,1)} %all-to-all-done.2), kind=kOutput, calls=%fused_computation.13 | convolution fusion | flops 34695282688 | bytes 176160768 | tf_op jit(solution)/shard_map/sekd,efd->eskf/dot_general | solution.py:54
  3271.0 48.5 %convolution_convert_fusion = bf16[8,4,1024,1024]{3,2,1,0:T(8,128)(2,1)} fusion(bf16[8,4,1024,512]{3,2,1,0:T(8,128)(2,1)} %fusion.6, bf16[8,1024,512]{2,1,0:T(8,128)(2,1)} %param.10), kind=kOutput, calls=%fused_computation.23 | convolution fusion | flops 34393292800 | bytes 109051904 | tf_op jit(solution)/shard_map/eskf,edf->eskd/dot_general | solution.py:58
  3319.5 44.3 %copy.27 = bf16[8,4,1024,1024]{3,2,0,1:T(8,128)(2,1)} copy(bf16[8,4,1024,1024]{3,2,1,0:T(8,128)(2,1)} %convolution_convert_fusion) | data formatting | bytes 134217728 | tf_op jit(solution)/shard_map/convert_element_type | solution.py:58
  3363.8 13.1 all-to-all-start.3
  3376.9 52.7 %fusion.21 = f32[8,512,1024]{2,1,0:T(8,128)} fusion(bf16[4,8,1024,1024]{3,2,1,0:T(8,128)(2,1)} %all-to-all-done.2, f32[8,4,1024,512]{3,2,1,0:T(8,128)} %fusion.7), kind=kOutput, calls=%fused_computation.35 | convolution fusion | flops 34510733312 | bytes 150994944 | tf_op jit(solution)/shard_map/eskf,sekd->efd/dot_general | solution.py:56
  3429.6 47.9 %fusion.18 = f32[8,1024,512]{2,1,0:T(8,128)} fusion(bf16[4,8,1024,1024]{3,2,1,0:T(8,128)(2,1)} %all_to_all.40, bf16[8,4,1024,512]{3,2,1,0:T(8,128)(2,1)} %fusion.6), kind=kOutput, calls=%fused_computation.34 | convolution fusion | flops 34359738368 | bytes 117440512 | tf_op jit(solution)/shard_map/sekd,eskf->edf/dot_general | solution.py:57
  3477.5 621.4 %all-to-all-done.3 = bf16[8,4,1024,1024]{3,2,0,1:T(8,128)(2,1)} async-done(((bf16[8,4,1024,1024]{3,2,0,1:T(8,128)(2,1)}), bf16[8,4,1024,1024]{3,2,0,1:T(8,128)(2,1)}, u32[]{:S(2)}, u32[]{:S(2)}) %all-to-all-start.3) | async-done | bytes 67108896 | tf_op jit(solution)/shard_map/all_to_all | solution.py:37
  4098.9 150.2 %gather_fusion.4 = bf16[8192,1024]{1,0:T(8,128)(2,1)} fusion(bf16[32768,1024]{1,0:T(8,128)(2,1)} %bitcast.46, s32[8192]{0:T(1024)S(1)} %copy-done.22), kind=kCustom, calls=%fused_computation.4 | custom fusion | bytes 33587200 | tf_op jit(solution)/shard_map/gather | solution.py:38
  (94 shorter events, 77.5 us)
Async XLA Ops:
  7.2 1341.7 %copy-start = (bf16[1024,32]{0,1:T(8,128)(2,1)S(1)}, bf16[1024,32]{0,1:T(8,128)(2,1)}, u32[]{:S(2)}) copy-start(bf16[1024,32]{0,1:T(8,128)(2,1)} %param.9) | copy-start | bytes 196612
  8.5 188.3 %copy-start.19 = (s32[32]{0:T(128)}, s32[32]{0:T(128)S(1)}, u32[]{:S(2)}) copy-start(s32[32]{0:T(128)S(1)} %sub.26) | copy-start | bytes 388
  16.1 180.7 %copy-start.1 = (s32[8192]{0:T(1024)}, s32[8192]{0:T(1024)S(1)}, u32[]{:S(2)}) copy-start(s32[8192]{0:T(1024)S(1)} %get-tuple-element.7) | copy-start | bytes 98308
  196.9 168.0 %copy-start.12 = (s32[32768]{0:T(1024)}, s32[32768]{0:T(1024)S(1)}, u32[]{:S(2)}) copy-start(s32[32768]{0:T(1024)S(1)} %broadcast_clamp_fusion.1) | copy-start | bytes 393220
  197.7 167.3 %copy-start.23 = (pred[4,8,1024]{2,1,0:T(8,128)(4,1)S(1)}, pred[4,8,1024]{2,1,0:T(8,128)(4,1)}, u32[]{:S(2)}) copy-start(pred[4,8,1024]{2,1,0:T(8,128)(4,1)} %iota_compare_fusion.1) | copy-start | bytes 98308
  1327.0 20.4 copy-start.20
  1327.0 33.6 copy-start.6
  1327.0 735.6 %all-to-all-start.1 = ((bf16[8,4,1024,1024]{3,2,0,1:T(8,128)(2,1)}), bf16[8,4,1024,1024]{3,2,0,1:T(8,128)(2,1)}, u32[]{:S(2)}, u32[]{:S(2)}) async-start(bf16[8,4,1024,1024]{3,2,0,1:T(8,128)(2,1)} %copy.25), calls=%async_computation.1 | async-start | bytes 134217728 | tf_op jit(solution)/shard_map/all_to_all | solution.py:37
  1381.6 681.0 %copy-start.21 = (s32[8192]{0:T(1024)}, s32[8192]{0:T(1024)S(1)}, u32[]{:S(2)}) copy-start(s32[8192]{0:T(1024)S(1)} %fusion.36) | copy-start | bytes 98308
  2212.8 26.0 copy-start.13
  2238.7 167.7 %copy-start.24 = (pred[4,8,1024]{2,1,0:T(8,128)(4,1)S(1)}, pred[4,8,1024]{2,1,0:T(8,128)(4,1)}, u32[]{:S(2)}) copy-start(pred[4,8,1024]{2,1,0:T(8,128)(4,1)} %iota_compare_fusion.1) | copy-start | bytes 98308
  2450.5 13.9 copy-start.4
  2450.5 13.9 copy-start.7
  2450.5 736.7 %all-to-all-start.2 = ((bf16[4,8,1024,1024]{3,2,1,0:T(8,128)(2,1)}), bf16[4,8,1024,1024]{3,2,1,0:T(8,128)(2,1)}, u32[]{:S(2)}, u32[]{:S(2)}) async-start(bf16[4,8,1024,1024]{3,2,1,0:T(8,128)(2,1)} %broadcast_select_fusion), calls=%async_computation.2 | async-start | bytes 134217728 | tf_op jit(solution)/shard_map/all_to_all | solution.py:34
  2463.7 1797.6 %all-reduce.4.cloned.1.call-start = ((), (), s32[]{:S(2)}) async-start(), calls=%async_computation.4 | async-start | bytes 262144 | tf_op jit(solution)/shard_map/psum | solution.py:67
  3363.8 735.1 %all-to-all-start.3 = ((bf16[8,4,1024,1024]{3,2,0,1:T(8,128)(2,1)}), bf16[8,4,1024,1024]{3,2,0,1:T(8,128)(2,1)}, u32[]{:S(2)}, u32[]{:S(2)}) async-start(bf16[8,4,1024,1024]{3,2,0,1:T(8,128)(2,1)} %copy.27), calls=%async_computation.3 | async-start | bytes 134217728 | tf_op jit(solution)/shard_map/all_to_all | solution.py:37
  3376.9 884.4 %all-reduce.6.cloned.1.call-start = ((), (), s32[]{:S(2)}) async-start(), calls=%async_computation.5 | async-start | bytes 67108864 | tf_op jit(solution)/shard_map/psum | solution.py:65
  3429.6 669.3 %copy-start.22 = (s32[8192]{0:T(1024)S(1)}, s32[8192]{0:T(1024)}, u32[]{:S(2)}) copy-start(s32[8192]{0:T(1024)} %copy-done.21) | copy-start | bytes 98308
  4098.9 150.2 %copy-start.5 = (f32[8192,32]{0,1:T(8,128)S(1)}, f32[8192,32]{0,1:T(8,128)}, u32[]{:S(2)}) copy-start(f32[8192,32]{0,1:T(8,128)} %copy-done.3) | copy-start | bytes 3145732
  4098.9 150.2 %copy-start.8 = (s32[8192]{0:T(1024)S(1)}, s32[8192]{0:T(1024)}, u32[]{:S(2)}) copy-start(s32[8192]{0:T(1024)} %param.8) | copy-start | bytes 98308
  4098.9 150.2 %copy-start.11 = (f32[8192]{0:T(1024)S(1)}, f32[8192]{0:T(1024)}, u32[]{:S(2)}) copy-start(f32[8192]{0:T(1024)} %copy-done.9) | copy-start | bytes 98308
  4098.9 150.2 %copy-start.16 = (f32[8192]{0:T(1024)S(1)}, f32[8192]{0:T(1024)}, u32[]{:S(2)}) copy-start(f32[8192]{0:T(1024)} %copy-done.14) | copy-start | bytes 98308
  4098.9 150.2 %copy-start.18 = (f32[8192]{0:T(1024)S(1)}, f32[8192]{0:T(1024)}, u32[]{:S(2)}) copy-start(f32[8192]{0:T(1024)} %copy-done.17) | copy-start | bytes 98308
  4261.3 23.7 copy-start.28
  (10 other events, 72.0 us)
Sparse Core Ops, SparseCore 0:
  2473.9 67.6 all-reduce.3
  3477.6 571.9 all-reduce.5
where the time goes:
time: 4310 us; the launch traced here: 4290 us
  waiting for transfers between devices  2020 us (47%)
  local copies, waits for them, and re-layouts  933 us (22%)
  blocking collectives  756 us (18%)
  matrix products  383 us (9%)
  other arithmetic  151 us (4%)
    all_to_all x2, waiting for transfers between devices, combine(): returned = lax.all_to_all(expert_rows, 'ep', 1, 0, tiled=True)  1300 us
    all_to_all x1, blocking collectives, dispatch(): return lax.all_to_all(picked, 'ep', 0, 0, tiled=True)  756 us
    all_to_all x1, waiting for transfers between devices, dispatch(): return lax.all_to_all(picked, 'ep', 0, 0, tiled=True)  713 us
    gather x2, local copies, waits for them, and re-layouts, dispatch(): tok_rows[src_tok]  335 us
    gather x2, local copies, waits for them, and re-layouts, combine(): return returned.reshape(n_experts * cap_rows, d_model)[slot_tok]  300 us
    gather x2, local copies, waits for them, and re-layouts, local_step(): sort_order[jnp.minimum(expert_start[:, None] + slot_k[None, :], tok_count...  181 us
    select_n x2, other arithmetic, dispatch(): jnp.where(slot_valid[:, :, None], tok_rows[src_tok], jnp.zeros((), tok_ro...  88 us
  transfers between devices with their start and end apart: 5, of which 3 were waited for; matrix products, arithmetic and copies ran while one was open for 11% of the time, Pallas kernels for 0%

commit v1 on v0

v1 whole, which is shorter than its diff:
```python
import functools

import jax
import jax.numpy as jnp
from jax import lax
from jax.experimental import pallas as pl
from jax.experimental.pallas import tpu as pltpu
from jax.sharding import PartitionSpec as P

ROWS = 256
ALIGN = 16
PIECES = (256, 128, 64, 32, 16)
GELU_C = 0.7978845608028654
GELU_A = 0.044715


def chunk_tables(counts, starts):
    calls, n_exp = counts.shape
    cap = n_exp * (1024 // ROWS)
    per = (counts + ROWS - 1) // ROWS
    end = jnp.cumsum(per, axis=1)
    begin = end - per
    c = jnp.arange(cap, dtype=jnp.int32)
    e = jnp.sum((c[None, :, None] >= end[:, None, :]).astype(jnp.int32), axis=2)
    hot = (e[:, :, None] == jnp.arange(n_exp, dtype=jnp.int32)).astype(jnp.int32)
    pick = lambda v: jnp.sum(hot * v[:, None, :], axis=2)
    j = c[None, :] - pick(begin)
    start = pick(starts) + j * ROWS
    n = jnp.clip(pick(counts) - j * ROWS, 0, ROWS)
    bounds = jnp.concatenate([begin, jnp.broadcast_to(end[:, -1:], (calls, cap - n_exp))], axis=1)
    return jnp.stack([jnp.where(n > 0, start, 0), n, bounds], axis=1)


def ffn_kernel(n_init, has_prev, tab, x_hbm, dy_hbm, w1, w2, *rest):
    rest = list(rest)
    inits = rest[: 2 * n_init]
    rest = rest[2 * n_init:]
    if has_prev:
        rest = rest[2:]
    dw1, dw2, y_hbm, dx_hbm, xb, dyb, yb, dxb, isem, osem = rest
    e = pl.program_id(0)
    n_exp = pl.num_programs(0)
    total = tab[2, n_exp]

    def pieces(ci, body):
        start = tab[0, ci]
        n = tab[1, ci]
        rows = (n + ALIGN - 1) & -ALIGN
        off = jnp.int32(0)
        for size in PIECES:
            has = (rows & size) != 0

            @pl.when(has)
            def _(off=off, size=size):
                body(pl.ds(pl.multiple_of(start + off, ALIGN), size), pl.ds(pl.multiple_of(off, ALIGN), size))

            off = off + jnp.where(has, size, 0)

    def load(ci, sl, act):
        def body(h, v):
            act(pltpu.make_async_copy(x_hbm.at[h], xb.at[sl, v], isem.at[0, sl]))
            act(pltpu.make_async_copy(dy_hbm.at[h], dyb.at[sl, v], isem.at[1, sl]))
        pieces(ci, body)

    def store(ci, sl, act):
        def body(h, v):
            act(pltpu.make_async_copy(yb.at[sl, v], y_hbm.at[h], osem.at[0, sl]))
            act(pltpu.make_async_copy(dxb.at[sl, v], dx_hbm.at[h], osem.at[1, sl]))
        pieces(ci, body)

    start_op = lambda d: d.start()
    wait_op = lambda d: d.wait()

    @pl.when((e == 0) & (total > 0))
    def _():
        load(0, 0, start_op)

    if n_init == 2:
        dw1[...] = inits[0][...] + inits[2][...]
        dw2[...] = inits[1][...] + inits[3][...]
    elif n_init == 1:
        dw1[...] = inits[0][...]
        dw2[...] = inits[1][...]
    else:
        dw1[...] = jnp.zeros_like(dw1)
        dw2[...] = jnp.zeros_like(dw2)

    @pl.loop(tab[2, e], tab[2, e + 1])
    def _(c):
        slot = lax.rem(c, 2)

        @pl.when(c + 1 < total)
        def _():
            load(c + 1, 1 - slot, start_op)

        load(c, slot, wait_op)

        @pl.when(c >= 2)
        def _():
            store(c - 2, slot, wait_op)

        keep = lax.broadcasted_iota(jnp.int32, (ROWS, 1), 0) < tab[1, c]
        x = jnp.where(keep, xb[slot], jnp.zeros((), jnp.bfloat16))
        dy = jnp.where(keep, dyb[slot], jnp.zeros((), jnp.bfloat16))
        a = jnp.dot(x, w1[0], preferred_element_type=jnp.float32)
        a2 = a * a
        t = jnp.tanh(GELU_C * (a + GELU_A * (a2 * a)))
        cdf = 0.5 * (1.0 + t)
        h = (a * cdf).astype(jnp.bfloat16)
        yb[slot] = jnp.dot(h, w2[0], preferred_element_type=jnp.float32).astype(jnp.bfloat16)
        dh = lax.dot_general(dy, w2[0], (((1,), (1,)), ((), ())), preferred_element_type=jnp.float32)
        slope = cdf + 0.5 * a * ((1.0 - t * t) * (GELU_C * (1.0 + 3.0 * GELU_A * a2)))
        da = (dh * slope).astype(jnp.bfloat16)
        dxb[slot] = lax.dot_general(da, w1[0], (((1,), (1,)), ((), ())), preferred_element_type=jnp.float32).astype(jnp.bfloat16)
        store(c, slot, start_op)
        dw2[0] += lax.dot_general(h, dy, (((0,), (0,)), ((), ())), preferred_element_type=jnp.float32)
        dw1[0] += lax.dot_general(x, da, (((0,), (0,)), ((), ())), preferred_element_type=jnp.float32)

    @pl.when(e == n_exp - 1)
    def _():
        for back in (2, 1):
            @pl.when(total >= back)
            def _(back=back):
                store(total - back, lax.rem(total - back, 2), wait_op)


def ffn(tab, x, dy, w1, w2, init=(), prev=None):
    n_rows, d = x.shape
    n_exp, _, f = w1.shape
    per_expert = lambda e, t: (e, 0, 0)
    any_spec = pl.BlockSpec(memory_space=pl.ANY)
    w_specs = [pl.BlockSpec((1, d, f), per_expert), pl.BlockSpec((1, f, d), per_expert)]
    args = [x, dy, w1, w2]
    specs = [any_spec, any_spec] + w_specs
    alias = {}
    if init:
        alias.update({1 + len(args): 0, 2 + len(args): 1})
    for pair in init:
        args += list(pair)
        specs += w_specs
    if prev is not None:
        alias.update({1 + len(args): 2, 2 + len(args): 3})
        args += list(prev)
        specs += [any_spec, any_spec]
    return pl.pallas_call(
        functools.partial(ffn_kernel, len(init), prev is not None),
        grid_spec=pltpu.PrefetchScalarGridSpec(
            num_scalar_prefetch=1,
            grid=(n_exp,),
            in_specs=specs,
            out_specs=w_specs + [any_spec, any_spec],
            scratch_shapes=[pltpu.VMEM((2, ROWS, d), jnp.bfloat16)] * 4 + [pltpu.SemaphoreType.DMA((2, 2))] * 2,
        ),
        out_shape=[
            jax.ShapeDtypeStruct((n_exp, d, f), jnp.float32),
            jax.ShapeDtypeStruct((n_exp, f, d), jnp.float32),
            jax.ShapeDtypeStruct((n_rows, d), jnp.bfloat16),
            jax.ShapeDtypeStruct((n_rows, d), jnp.bfloat16),
        ],
        input_output_aliases=alias,
        compiler_params=pltpu.CompilerParams(dimension_semantics=("arbitrary",), vmem_limit_bytes=58 * 1024 * 1024),
        cost_estimate=pl.CostEstimate(flops=12 * 4096 * d * f, bytes_accessed=96 * 1024 * 1024, transcendentals=4096 * f),
    )(tab, *args)


def solution(mesh):
    tok_spec = P(('dp', 'ep'), None)
    idx_spec = P(('dp', 'ep'))
    rep_spec = P(None, None)
    exp_spec = P('ep', None, None)
    ep_size = mesh.shape['ep']
    swap_x = [(i, i ^ 2) for i in range(ep_size)]
    swap_core = [(i, i ^ 1) for i in range(ep_size)]

    def local_step(x_loc, gy_loc, idx_loc, w_gate, w_up, w_down):
        tok, d = x_loc.shape
        n_exp = w_gate.shape[1]
        per_dev = w_up.shape[0]
        half = n_exp // 2
        slots = tok + n_exp * ALIGN
        levels = (4960, tok + half * ALIGN)
        ep = lax.axis_index('ep')
        dp = lax.axis_index('dp')
        w_up_s = lax.ppermute(w_up, 'ep', swap_core)
        w_down_s = lax.ppermute(w_down, 'ep', swap_core)

        key = ((idx_loc // per_dev) ^ (ep ^ 1)) * per_dev + idx_loc % per_dev
        lanes = jnp.arange(n_exp, dtype=jnp.int32)
        count = jnp.sum((key[:, None] == lanes[None, :]).astype(jnp.int32), axis=0)
        all_count = lax.all_gather(count, ('dp', 'ep'))

        def gap(k):
            return jnp.where(k >= half, k + 1, k)

        fill = jnp.arange(ALIGN, dtype=jnp.int32)
        fill_cls = jnp.where(fill[None, :] < ((-count) % ALIGN)[:, None], gap(lanes)[:, None], half).reshape(-1)
        cls = jnp.concatenate([gap(key), fill_cls])
        ids = jnp.arange(slots, dtype=jnp.int32)
        order = lax.sort(cls * 16384 + ids, is_stable=False) % 16384
        slot_of = lax.sort(order * 16384 + ids, is_stable=False)[:tok] % 16384
        src = jnp.where(order < tok, order, 0)
        xs = x_loc[src]

        logit = jnp.dot(x_loc, w_gate, preferred_element_type=jnp.float32)
        prob = jax.nn.softmax(logit, axis=-1)
        onehot = idx_loc[:, None] == lanes[None, :]
        gate = n_exp * jnp.sum(jnp.where(onehot, prob, 0.0), axis=1)
        dy = (gate[:, None] * gy_loc.astype(jnp.float32)).astype(jnp.bfloat16)
        dys = dy[src]

        def padded(cnt):
            return (cnt + ALIGN - 1) // ALIGN * ALIGN

        all_pad = padded(all_count)
        tail_need = jnp.max(jnp.sum(all_pad[:, half:], axis=1))
        level = sum((tail_need > c).astype(jnp.int32) for c in levels[:-1])
        pad_own = padded(count)
        head_start = jnp.cumsum(pad_own[:half]) - pad_own[:half]
        head_total = jnp.sum(pad_own[:half])
        p_count = lax.dynamic_index_in_dim(all_count, dp * ep_size + (ep ^ 2), 0, keepdims=False)[half:]
        p_pad = padded(p_count)
        tail_start = jnp.cumsum(p_pad) - p_pad - jnp.sum(p_pad)

        def run(cap, ops):
            xs, dys, slot_of, head_start, tail_start, count, p_count, w_up, w_down, w_up_s, w_down_s, x_loc, gy_loc, gate, prob, onehot, w_gate = ops
            rx = lax.ppermute(xs[slots - cap:], 'ep', swap_x)
            rdy = lax.ppermute(dys[slots - cap:], 'ep', swap_x)
            k = per_dev
            tab = chunk_tables(
                jnp.stack([count[:k], count[k:2 * k], p_count[:k], p_count[k:]]),
                jnp.stack([head_start[:k], head_start[k:], cap + tail_start[:k], cap + tail_start[k:]]),
            )
            dws1, dws2, yo, dxo = ffn(tab[0], xs, dys, w_up_s, w_down_s)
            dws1, dws2, yp, dxp = ffn(tab[2], rx, rdy, w_up_s, w_down_s, init=((dws1, dws2),))
            add1 = lax.ppermute(dws1, 'ep', swap_core)
            add2 = lax.ppermute(dws2, 'ep', swap_core)
            dwo1, dwo2, yo, dxo = ffn(tab[1], xs, dys, w_up, w_down, prev=(yo, dxo))
            dwo1, dwo2, yp, dxp = ffn(tab[3], rx, rdy, w_up, w_down, init=((dwo1, dwo2), (add1, add2)), prev=(yp, dxp))
            ry = lax.ppermute(yp, 'ep', swap_x)
            rdx = lax.ppermute(dxp, 'ep', swap_x)
            g_up = lax.psum(dwo1, 'dp')
            g_down = lax.psum(dwo2, 'dp')
            gy_full = gy_loc.astype(jnp.float32)
            in_head = (jnp.arange(slots, dtype=jnp.int32) < head_total)[:, None]
            merge = lambda own, ret: jnp.where(in_head, own, jnp.pad(ret, ((slots - cap, 0), (0, 0))))
            y_tok = merge(yo, ry)[slot_of].astype(jnp.float32)
            moe_out = (gate[:, None] * y_tok).astype(jnp.bfloat16)
            d_gate = jnp.sum(gy_full * y_tok, axis=1)
            d_logit = ((d_gate * gate)[:, None] * (onehot.astype(jnp.float32) - prob)).astype(jnp.bfloat16)
            g_gate = jnp.einsum('td,te->de', x_loc, d_logit, preferred_element_type=jnp.float32)
            for axis, flip in (('ep', 1), ('ep', 2), ('dp', 1), ('dp', 2)):
                g_gate = g_gate + lax.ppermute(g_gate, axis, [(i, i ^ flip) for i in range(mesh.shape[axis])])
            dx_exp = merge(dxo, rdx)[slot_of]
            dx_router = jnp.einsum('te,de->td', d_logit, w_gate, preferred_element_type=jnp.float32)
            g_x = (dx_exp.astype(jnp.float32) + dx_router).astype(jnp.bfloat16)
            return moe_out, g_x, g_up, g_down, g_gate

        ops = (xs, dys, slot_of, head_start, tail_start, count, p_count, w_up, w_down, w_up_s, w_down_s, x_loc, gy_loc, gate, prob, onehot, w_gate)
        return lax.switch(level, [functools.partial(run, c) for c in levels], ops)

    return jax.shard_map(local_step, mesh=mesh, in_specs=(tok_spec, tok_spec, idx_spec, rep_spec, exp_spec, exp_spec), out_specs=(tok_spec, tok_spec, exp_spec, exp_spec, rep_spec), check_vma=False)
```

time: 4310 us -> 1410 us (0.33)
  waiting for transfers between devices: 2020 us -> 793 us
  blocking collectives: 756 us -> 50.4 us
  local copies, waits for them, and re-layouts: 933 us -> 237 us
  matrix products: 383 us -> 31.9 us
  Pallas kernels: 0 us -> 149 us
  other arithmetic: 151 us -> 85.3 us
    all_to_all x3 -> x0, waiting for transfers between devices: 2020 us -> none  [the longest x2 1300 us: combine(): returned = lax.all_to_all(expert_rows, 'ep', 1, 0, tiled=True)]
    ppermute x0 -> x12, waiting for transfers between devices: none -> 793 us  [the longest x1 216 us: run(): rdy = lax.ppermute(dys[slots - cap:], 'ep', swap_x)]
    all_to_all x1 -> x0, blocking collectives: 756 us -> none  [dispatch(): return lax.all_to_all(picked, 'ep', 0, 0, tiled=True)]
    gather x8 -> x4, local copies, waits for them, and re-layouts: 817 us -> 189 us  [the longest x1 48.9 us: run(): dx_exp = merge(dxo, rdx)[slot_of]]
    dot_general x9 -> x3, matrix products: 383 us -> 31.9 us  [the longest x1 12.8 us: run(): jnp.einsum('te,de->td', d_logit, w_gate, preferred_element_type=jnp.float32)]
    pallas_call x0 -> x4, Pallas kernels: none -> 149 us  [ffn(): pl.pallas_call(functools.partial(ffn_kernel, len(init), prev is not None)...]
    convert_element_type x2 -> x0, local copies, waits for them, and re-layouts: 88.6 us -> none  [the longest x1 44.3 us: local_step(): jnp.einsum('eskf,edf->eskd', d_pre, w_up, preferred_element_type=jnp.floa...]
    select_n x2 -> x7, other arithmetic: 88 us -> 34.9 us  [the longest x1 34 us: run(): jnp.where(in_head, own, jnp.pad(ret, ((slots - cap, 0), (0, 0))))]
  transfers between devices with their start and end apart: 5 -> 13, of which waited for: 3 -> 7; matrix products, arithmetic and copies ran while one was open for 11% -> 20% of each run, Pallas kernels for 0% -> 4%
where the time goes in v1:
time: 1410 us
  waiting for transfers between devices  793 us (56%)
  local copies, waits for them, and re-layouts  237 us (17%)
  Pallas kernels  149 us (11%)
  other arithmetic  85.3 us (6%)
  blocking collectives  50.4 us (4%)
  starting transfers between devices  36.1 us (3%)
  matrix products  31.9 us (2%)
  between operations  15.3 us (1%)
    ppermute x1, waiting for transfers between devices, run(): rdy = lax.ppermute(dys[slots - cap:], 'ep', swap_x)  216 us
    ppermute x1, waiting for transfers between devices, run(): rdx = lax.ppermute(dxp, 'ep', swap_x)  215 us
    ppermute x1, waiting for transfers between devices, run(): ry = lax.ppermute(yp, 'ep', swap_x)  211 us
    pallas_call x4, Pallas kernels, ffn(): pl.pallas_call(functools.partial(ffn_kernel, len(init), prev is not None)...  149 us
    ppermute x1, waiting for transfers between devices, run(): rx = lax.ppermute(xs[slots - cap:], 'ep', swap_x)  132 us
    unnamed x1, blocking collectives  50.4 us
    gather x1, local copies, waits for them, and re-layouts, run(): dx_exp = merge(dxo, rdx)[slot_of]  48.9 us
    gather x1, local copies, waits for them, and re-layouts, run(): y_tok = merge(yo, ry)[slot_of].astype(jnp.float32)  48.8 us
  transfers between devices with their start and end apart: 13, of which 7 were waited for; matrix products, arithmetic and copies ran while one was open for 20% of the time, Pallas kernels for 4%

profile of v1, /device:TPU:0, one launch (start us, length us, event | category | flops | bytes accessed | tf_op | source)
XLA Modules:
  0.0 1408.1 jit_solution(9701944443467157744)
XLA Ops:
  9.3 50.4 %all-reduce.4 = s32[512]{0:T(512)S(1)} all-reduce(s32[512]{0:T(512)S(1)} %dynamic-update-slice), channel_id=2, replica_groups=mesh['dp'=4,'ep'=4] {'dp','ep'}, use_global_device_ids=true, to_apply=%add.4 | all-reduce | flops 512 | bytes 4096
  74.5 10.9 fusion.56
  96.2 1281.9 %conditional.4 = (f32[8,1024,512]{2,1,0:T(8,128)}, f32[8,512,1024]{2,1,0:T(8,128)}, f32[1024,32]{0,1:T(8,128)S(1)}, bf16[8192,1024]{1,0:T(8,128)(2,1)}, bf16[8192,1024]{1,0:T(8,128)(2,1)}) conditional(s32[]{:T(128)} %clamp.27, (s32[32]{0:T(128)S(1)}, s32[16]{0:T(128)S(1)}, s32[16,1]{1,0:T(8,128)S(1)}, s32[16]{0:T(128)S(1)}, ...), branch_computations={%region_10.21_spmd, %region_21.32_spmd} | conditional | flops 104265441280 | bytes 1516242816
  96.2 9.0 all-reduce.10.cloned.1.call-start
  105.3 45.8 %gather_fusion = bf16[8704,1024]{1,0:T(8,128)(2,1)} fusion(bf16[8192,1024]{1,0:T(8,128)(2,1)} %get-tuple-element.162, s32[9216]{0:T(1024)S(1)} %pad_clamp_fusion), kind=kCustom, calls=%fused_computation | custom fusion | bytes 35686400 | tf_op jit(solution)/shard_map/gather | solution.py:202
  151.1 9.1 slice.129
  162.5 45.8 %gather_fusion.1 = bf16[8704,1024]{1,0:T(8,128)(2,1)} fusion(bf16[8192,1024]{1,0:T(8,128)(2,1)} %get-tuple-element.164, s32[9216]{0:T(1024)S(1)} %pad_clamp_fusion), kind=kCustom, calls=%fused_computation.1 | custom fusion | bytes 35686400 | tf_op jit(solution)/shard_map/gather | solution.py:209
  208.3 9.0 slice.130
  221.0 28.3 %branch_0_fun.4 = (f32[8,1024,512]{2,1,0:T(8,128)}, f32[8,512,1024]{2,1,0:T(8,128)}, bf16[8704,1024]{1,0:T(8,128)(2,1)}, bf16[8704,1024]{1,0:T(8,128)(2,1)}) custom-call(s32[3,32]{1,0:T(4,128)} %bitcast.154, bf16[8704,1024]{1,0:T(8,128)(2,1)} %gather_fusion, bf16[8704,1024]{1,0:T(8,128)(2,1)} %gather_fusion.1, bf16[8,1024,512]{2,1,0:T(8,128)(2,1)} %get-tuple-element.167.w1, ...), custom_call_target="tpu_custom_call" | custom-call | flops 25769803776 | bytes 100663296 | tf_op jit(solution)/shard_map/cond/branch_0_fun/pallas_call | solution.py:145
  249.3 132.4 %collective-permute-done.x_hbm = bf16[4960,1024]{1,0:T(8,128)(2,1)} collective-permute-done((bf16[4960,1024]{1,0:T(8,128)(2,1)}, bf16[4960,1024]{1,0:T(8,128)(2,1)}, u32[]{:S(2)}, u32[]{:S(2)}) %collective-permute-start) | collective-permute-done | bytes 10158112 | tf_op jit(solution)/shard_map/cond/branch_0_fun/ppermute | solution.py:226
  381.7 216.1 %collective-permute-done.1.dy_hbm = bf16[4960,1024]{1,0:T(8,128)(2,1)} collective-permute-done((bf16[4960,1024]{1,0:T(8,128)(2,1)}, bf16[4960,1024]{1,0:T(8,128)(2,1)}, u32[]{:S(2)}, u32[]{:S(2)}) %collective-permute-start.1) | collective-permute-done | bytes 10158112 | tf_op jit(solution)/shard_map/cond/branch_0_fun/ppermute | solution.py:227
  597.8 38.9 %branch_0_fun.6 = (f32[8,1024,512]{2,1,0:T(8,128)}, f32[8,512,1024]{2,1,0:T(8,128)}, bf16[4960,1024]{1,0:T(8,128)(2,1)}, bf16[4960,1024]{1,0:T(8,128)(2,1)}) custom-call(s32[3,32]{1,0:T(4,128)} %bitcast.150, bf16[4960,1024]{1,0:T(8,128)(2,1)} %collective-permute-done.x_hbm, ...), custom_call_target="tpu_custom_call", output_to_operand_aliasing={{0}: (5, {}), {1}: (6, {})} | custom-call | flops 25769803776 | bytes 100663296 | tf_op jit(solution)/shard_map/cond/branch_0_fun/pallas_call | solution.py:145
  643.1 35.0 %branch_0_fun.5 = (f32[8,1024,512]{2,1,0:T(8,128)}, f32[8,512,1024]{2,1,0:T(8,128)}, bf16[8704,1024]{1,0:T(8,128)(2,1)}, bf16[8704,1024]{1,0:T(8,128)(2,1)}) custom-call(s32[3,32]{1,0:T(4,128)} %bitcast.152, bf16[8704,1024]{1,0:T(8,128)(2,1)} %gather_fusion, bf16[8704,1024]{1,0:T(8,128)(2,1)} %gather_fusion.1, ...), custom_call_target="tpu_custom_call", output_to_operand_aliasing={{2}: (5, {}), {3}: (6, {})} | custom-call | flops 25769803776 | bytes 100663296 | tf_op jit(solution)/shard_map/cond/branch_0_fun/pallas_call | solution.py:145
  678.1 12.6 collective-permute-done.3.rest_3_
  690.7 46.4 %branch_0_fun.7 = (f32[8,1024,512]{2,1,0:T(8,128)}, f32[8,512,1024]{2,1,0:T(8,128)}, bf16[4960,1024]{1,0:T(8,128)(2,1)}, bf16[4960,1024]{1,0:T(8,128)(2,1)}) custom-call(s32[3,32]{1,0:T(4,128)} %bitcast.148, bf16[4960,1024]{1,0:T(8,128)(2,1)} %collective-permute-done.x_hbm, ...), custom_call_target="tpu_custom_call", output_to_operand_aliasing={{0}: (5, {}), {1}: (6, {}), {2}: (9, {}), {3}: (10, {})} | custom-call | flops 25769803776 | bytes 100663296 | tf_op jit(solution)/shard_map/cond/branch_0_fun/pallas_call | solution.py:145
  737.1 14.9 %collective-permute-start.9 = (bf16[4960,1024]{1,0:T(8,128)(2,1)}, bf16[4960,1024]{1,0:T(8,128)(2,1)}, u32[]{:S(2)}, u32[]{:S(2)}) collective-permute-start(bf16[4960,1024]{1,0:T(8,128)(2,1)} %get-tuple-element.190), channel_id=1, source_target_pairs={{0,2},{1,3},{2,0},{3,1},{4,6},{5,7},{6,4},{7,5},{8,10},{9,11},{10,... | collective-permute-start | bytes 30474248 | tf_op jit(solution)/shard_map/cond/branch_0_fun/ppermute | solution.py:240
  756.6 214.6 %collective-permute-done.9 = bf16[4960,1024]{1,0:T(8,128)(2,1)} collective-permute-done((bf16[4960,1024]{1,0:T(8,128)(2,1)}, bf16[4960,1024]{1,0:T(8,128)(2,1)}, u32[]{:S(2)}, u32[]{:S(2)}) %collective-permute-start.9) | collective-permute-done | bytes 10158112 | tf_op jit(solution)/shard_map/cond/branch_0_fun/ppermute | solution.py:240
  971.2 211.3 %collective-permute-done.4 = bf16[4960,1024]{1,0:T(8,128)(2,1)} collective-permute-done((bf16[4960,1024]{1,0:T(8,128)(2,1)}, bf16[4960,1024]{1,0:T(8,128)(2,1)}, u32[]{:S(2)}, u32[]{:S(2)}) %collective-permute-start.4) | collective-permute-done | bytes 10158112 | tf_op jit(solution)/shard_map/cond/branch_0_fun/ppermute | solution.py:239
  1182.5 34.0 %pad_select_fusion = (bf16[8704,1024]{1,0:T(8,128)(2,1)}, bf16[8704,1024]{1,0:T(8,128)(2,1)}) fusion(bf16[8704,1024]{1,0:T(8,128)(2,1)} %get-tuple-element.189, bf16[4960,1024]{1,0:T(8,128)(2,1)} %collective-permute-done.9, pred[8704]{0:T(1024)(128)(4,1)S(1)} %iota_compare_fusion, bf16[8704,1024]{1,0:T(8,128)(2,1)} %get-tuple-element.182, ...), kind=kLoop, calls=%fused_computation.12 | loop fusion | flops 17825792 | bytes 91628032 | tf_op jit(solution)/shard_map/cond/branch_0_fun/jit(_where)/select_n | solution.py:245
  1216.4 48.8 %gather_fusion.2 = bf16[8192,1024]{1,0:T(8,128)(2,1)} fusion(bf16[8704,1024]{1,0:T(8,128)(2,1)} %get-tuple-element.553, s32[8192]{0:T(1024)S(1)} %fusion.1), kind=kCustom, calls=%fused_computation.2 | custom fusion | bytes 33587200 | tf_op jit(solution)/shard_map/cond/branch_0_fun/gather | solution.py:246
  1265.3 15.6 %fusion = f32[8192]{0:T(1024)S(1)} fusion(bf16[8192,1024]{1,0:T(8,128)(2,1)} %gather_fusion.2, bf16[8192,1024]{1,0:T(8,128)(2,1)} %get-tuple-element.181), kind=kLoop, calls=%fused_computation.10 | loop fusion | flops 33546240 | bytes 33587200 | tf_op jit(solution)/shard_map/cond/branch_0_fun/reduce_sum | solution.py:248
  1305.3 48.9 %gather_fusion.3 = bf16[8192,1024]{1,0:T(8,128)(2,1)} fusion(bf16[8704,1024]{1,0:T(8,128)(2,1)} %get-tuple-element.552, s32[8192]{0:T(1024)S(1)} %fusion.1), kind=kCustom, calls=%fused_computation.3 | custom fusion | bytes 33587200 | tf_op jit(solution)/shard_map/cond/branch_0_fun/gather | solution.py:253
  1355.7 12.8 convert_add_fusion
  1378.2 12.7 copy.121
  (126 shorter events, 79.8 us)
Async XLA Ops:
  7.2 78.7 %copy-start.15 = (s32[8192]{0:T(1024)S(1)}, s32[8192]{0:T(1024)}, u32[]{:S(2)}) copy-start(s32[8192]{0:T(1024)} %param.10) | copy-start | bytes 98308
  7.2 89.0 %collective-permute-start.20 = (bf16[8,1024,512]{2,1,0:T(8,128)(2,1)}, bf16[8,1024,512]{2,1,0:T(8,128)(2,1)}, u32[]{:S(2)}, u32[]{:S(2)}) collective-permute-start(bf16[8,1024,512]{2,1,0:T(8,128)(2,1)} %param.12), channel_id=1, source_target_pairs={{0,1},{1,0},{2,3},{3,2},{4,5},{5,4},{6,7},{7,6},{8,9},{9,8},{10,11... | collective-permute-start | bytes 25165832 | tf_op jit(solution)/shard_map/ppermute | solution.py:184
  8.0 88.2 %collective-permute-start.21 = (bf16[8,512,1024]{2,1,0:T(8,128)(2,1)}, bf16[8,512,1024]{2,1,0:T(8,128)(2,1)}, u32[]{:S(2)}, u32[]{:S(2)}) collective-permute-start(bf16[8,512,1024]{2,1,0:T(8,128)(2,1)} %param.13), channel_id=1, source_target_pairs={{0,1},{1,0},{2,3},{3,2},{4,5},{5,4},{6,7},{7,6},{8,9},{9,8},{10,11... | collective-permute-start | bytes 25165832 | tf_op jit(solution)/shard_map/ppermute | solution.py:185
  96.2 1272.4 %all-reduce.10.cloned.1.call-start = ((), (), s32[]{:S(2)}) async-start(), calls=%async_computation | async-start | bytes 67108864 | tf_op jit(solution)/shard_map/cond/branch_0_fun/psum | solution.py:241
  160.2 221.5 %collective-permute-start = (bf16[4960,1024]{1,0:T(8,128)(2,1)}, bf16[4960,1024]{1,0:T(8,128)(2,1)}, u32[]{:S(2)}, u32[]{:S(2)}) collective-permute-start(bf16[4960,1024]{1,0:T(8,128)(2,1)} %slice.129), channel_id=1, source_target_pairs={{0,2},{1,3},{2,0},{3,1},{4,6},{5,7},{6,4},{7,5},{8,10},{9,11},{10,... | collective-permute-start | bytes 30474248 | tf_op jit(solution)/shard_map/cond/branch_0_fun/ppermute | solution.py:226
  217.3 380.5 %collective-permute-start.1 = (bf16[4960,1024]{1,0:T(8,128)(2,1)}, bf16[4960,1024]{1,0:T(8,128)(2,1)}, u32[]{:S(2)}, u32[]{:S(2)}) collective-permute-start(bf16[4960,1024]{1,0:T(8,128)(2,1)} %slice.130), channel_id=1, source_target_pairs={{0,2},{1,3},{2,0},{3,1},{4,6},{5,7},{6,4},{7,5},{8,10},{9,11},{10,... | collective-permute-start | bytes 30474248 | tf_op jit(solution)/shard_map/cond/branch_0_fun/ppermute | solution.py:227
  636.7 41.4 %collective-permute-start.2 = (f32[8,1024,512]{2,1,0:T(8,128)}, f32[8,1024,512]{2,1,0:T(8,128)}, u32[]{:S(2)}, u32[]{:S(2)}) collective-permute-start(f32[8,1024,512]{2,1,0:T(8,128)} %get-tuple-element.175), channel_id=1, source_target_pairs={{0,1},{1,0},{2,3},{3,2},{4,5},{5,4},{6,7},{7,6},{8,9},{9,8},{10,11... | collective-permute-start | bytes 50331656 | tf_op jit(solution)/shard_map/cond/branch_0_fun/ppermute | solution.py:235
  641.9 48.8 %collective-permute-start.3 = (f32[8,512,1024]{2,1,0:T(8,128)}, f32[8,512,1024]{2,1,0:T(8,128)}, u32[]{:S(2)}, u32[]{:S(2)}) collective-permute-start(f32[8,512,1024]{2,1,0:T(8,128)} %get-tuple-element.176), channel_id=1, source_target_pairs={{0,1},{1,0},{2,3},{3,2},{4,5},{5,4},{6,7},{7,6},{8,9},{9,8},{10,11... | collective-permute-start | bytes 50331656 | tf_op jit(solution)/shard_map/cond/branch_0_fun/ppermute | solution.py:236
  737.1 17.6 %copy-start.6 = (pred[8192,32]{0,1:T(32,128)(4,1)S(1)}, pred[8192,32]{0,1:T(32,128)(4,1)}, u32[]{:S(2)}) copy-start(pred[8192,32]{0,1:T(32,128)(4,1)} %get-tuple-element.470) | copy-start | bytes 786436
  737.1 19.5 %copy-start.8 = (s32[8192]{0:T(1024)S(1)}, s32[8192]{0:T(1024)}, u32[]{:S(2)}) copy-start(s32[8192]{0:T(1024)} %get-tuple-element.253) | copy-start | bytes 98308
  737.1 19.5 %copy-start.17 = (pred[8192]{0:T(1024)(128)(4,1)S(1)}, pred[8192]{0:T(1024)(128)(4,1)}, u32[]{:S(2)}) copy-start(pred[8192]{0:T(1024)(128)(4,1)} %get-tuple-element.251) | copy-start | bytes 24580
  737.1 234.1 %collective-permute-start.9 = (bf16[4960,1024]{1,0:T(8,128)(2,1)}, bf16[4960,1024]{1,0:T(8,128)(2,1)}, u32[]{:S(2)}, u32[]{:S(2)}) collective-permute-start(bf16[4960,1024]{1,0:T(8,128)(2,1)} %get-tuple-element.190), channel_id=1, source_target_pairs={{0,2},{1,3},{2,0},{3,1},{4,6},{5,7},{6,4},{7,5},{8,10},{9,11},{10,... | collective-permute-start | bytes 30474248 | tf_op jit(solution)/shard_map/cond/branch_0_fun/ppermute | solution.py:240
  752.0 430.5 %collective-permute-start.4 = (bf16[4960,1024]{1,0:T(8,128)(2,1)}, bf16[4960,1024]{1,0:T(8,128)(2,1)}, u32[]{:S(2)}, u32[]{:S(2)}) collective-permute-start(bf16[4960,1024]{1,0:T(8,128)(2,1)} %get-tuple-element.183), channel_id=1, source_target_pairs={{0,2},{1,3},{2,0},{3,1},{4,6},{5,7},{6,4},{7,5},{8,10},{9,11},{10,... | collective-permute-start | bytes 30474248 | tf_op jit(solution)/shard_map/cond/branch_0_fun/ppermute | solution.py:239
  1265.3 15.6 %copy-start.1 = (f32[8192,32]{1,0:T(8,128)S(1)}, f32[8192,32]{1,0:T(8,128)}, u32[]{:S(2)}) copy-start(f32[8192,32]{1,0:T(8,128)} %copy.56) | copy-start | bytes 3145732
  1265.3 32.4 %slice-start = ((s8[16777216]{0:T(1024)(128)(4,1)}), s8[4194304]{0:T(1024)(128)(4,1)S(1)}, s32[]{:S(2)}) async-start(s8[16777216]{0:T(1024)(128)(4,1)} %bitcast.144), calls=%async_computation.2 | async-start | bytes 8388608
  1265.3 32.4 %slice-start.1 = ((s8[16777216]{0:T(1024)(128)(4,1)}), s8[4194304]{0:T(1024)(128)(4,1)S(1)}, s32[]{:S(2)}) async-start(s8[16777216]{0:T(1024)(128)(4,1)} %bitcast.144), calls=%async_computation.3 | async-start | bytes 8388608
  1280.9 16.8 %slice-start.2 = ((s8[16777216]{0:T(1024)(128)(4,1)}), s8[4194304]{0:T(1024)(128)(4,1)S(1)}, s32[]{:S(2)}) async-start(s8[16777216]{0:T(1024)(128)(4,1)} %bitcast.144), calls=%async_computation.4 | async-start | bytes 8388608
  1280.9 16.8 %slice-start.3 = ((s8[16777216]{0:T(1024)(128)(4,1)}), s8[4194304]{0:T(1024)(128)(4,1)S(1)}, s32[]{:S(2)}) async-start(s8[16777216]{0:T(1024)(128)(4,1)} %bitcast.144), calls=%async_computation.5 | async-start | bytes 8388608
  1289.1 1.4 collective-permute-start.5
  1290.5 5.6 collective-permute-start.6
  1296.2 58.0 %collective-permute-start.7 = (f32[1024,32]{0,1:T(8,128)S(1)}, f32[1024,32]{0,1:T(8,128)S(1)}, u32[]{:S(2)}, u32[]{:S(2)}) collective-permute-start(f32[1024,32]{0,1:T(8,128)S(1)} %add.184), channel_id=1, source_target_pairs={{0,4},{4,0},{8,12},{12,8},{1,5},{5,1},{9,13},{13,9},{2,6},{6,2},{1... | collective-permute-start | bytes 393224 | tf_op jit(solution)/shard_map/cond/branch_0_fun/ppermute | solution.py:252
  1305.3 50.4 %copy-start.10 = (bf16[1024,32]{0,1:T(8,128)(2,1)S(1)}, bf16[1024,32]{0,1:T(8,128)(2,1)}, u32[]{:S(2)}) copy-start(bf16[1024,32]{0,1:T(8,128)(2,1)} %get-tuple-element.472) | copy-start | bytes 196612
  1354.2 14.4 %collective-permute-start.8 = (f32[1024,32]{0,1:T(8,128)S(1)}, f32[1024,32]{0,1:T(8,128)S(1)}, u32[]{:S(2)}, u32[]{:S(2)}) collective-permute-start(f32[1024,32]{0,1:T(8,128)S(1)} %add.185), channel_id=1, source_target_pairs={{0,8},{4,12},{8,0},{12,4},{1,9},{5,13},{9,1},{13,5},{2,10},{6,14},... | collective-permute-start | bytes 393224 | tf_op jit(solution)/shard_map/cond/branch_0_fun/ppermute | solution.py:252
  1378.2 16.5 %copy-start.3 = (f32[8,512,1024]{2,1,0:T(8,128)S(1)}, f32[8,512,1024]{2,1,0:T(8,128)}, u32[]{:S(2)}) copy-start(f32[8,512,1024]{2,1,0:T(8,128)} %get-tuple-element.629) | copy-start | bytes 50331652
  (5 other events, 66.5 us)
Sparse Core Ops, SparseCore 0:
  737.2 585.5 all-reduce.9
